TPU v7x, 32 devices: a whole 2x2x4 slice. The times are simulated.
32 devices in a mesh: groups: 2 (over y), tm: 4 (over z), chan: 4 (over x, core).
Axes of the slice: x: 2, y: 2, z: 4, core: 2. Of those that a mesh axis runs over, the one named last changes fastest.
Arguments:
- vis: bfloat16 [8, 128, 2, 128], P(('groups', 'chan'), 'tm'), parts along dimension 0, may hold values from -6 to 6
- row_weight: bfloat16 [8, 128, 128, 128], P(('groups', 'chan'), 'tm'), parts along dimension 0, may hold values from -4 to 4
- col_weight: bfloat16 [8, 128, 128, 256], P(('groups', 'chan'), 'tm'), parts along dimension 0, may hold values from -0.5 to 0.5
- w_bin: int32 [8, 128, 1], P(('groups', 'chan'), 'tm'), parts along dimension 0, may hold values from 0 to 3; in each aligned block of 32 rows (0 to 31, 32 to 63, ..., all dimensions but the last counted through in order) at most 16 rows name the same one
- tile_col: int32 [8, 128], P(('groups', 'chan'), 'tm'), parts along dimension 0, may hold values from 0 to 15
- w_kernel: bfloat16 [8, 512, 512], P(('groups', 'tm')), parts along dimension 0, may hold values from -0.25 to 0.25
Outputs:
- grid: float32 [8, 128, 16, 512], P(('groups', 'tm'), 'chan'), parts along dimension 0
There are 2 independent parts, one for each index of `groups`. A program takes and returns all parts, laid end to end along the dimension named above; each array names one. Nothing has to cross between parts.
Inputs may be any that keep to these rules, and one draw needn't show every extreme that they name: `w_bin`: within the blocks of one device (aligned blocks of 32 along the channel-group and block dimensions taken together), no w-plane is named more than 16 times, a bound that some block reaches.
All inputs are finite; a program needn't handle non-finite values.
Results may differ from a plain program's by a relative error of at most 0.0041.
Values may be sent and summed in bfloat16 or wider, within the bound.
A program may use at most 128 MiB of HBM per device.

v0:
```python
import jax
import jax.numpy as jnp
from jax import lax
from jax.sharding import PartitionSpec as P

QW = 256
GC = 4096


def grid_group(total, weighted, columns, targets):
    patch = jnp.einsum("ghkv,gvq->gkhq", weighted, columns, preferred_element_type=jnp.float32)
    flat = patch.reshape(patch.shape[0], -1)
    return total.at[targets].add(flat, mode="drop")


def weigh_rows(rows, visibility):
    return (
        rows.astype(jnp.float32)[:, None, :, :] * visibility.astype(jnp.float32)[:, :, None, :]
    ).astype(jnp.bfloat16)


def body(vis, row_weight, col_weight, w_bin, tile_col, w_kernel):
    planes = lax.axis_size("tm")
    count = vis.shape[1]
    rows_k = row_weight.shape[2]
    width_v = vis.shape[3]
    width_q = col_weight.shape[3]
    tile_count = GC // QW
    per_plane = 2 * count // planes
    slot_total = planes * per_plane
    turns = 4
    group_len = slot_total // turns
    bins = w_bin[0, :, 0]
    tiles = tile_col[0]
    member = (bins[:, None] == jnp.arange(planes, dtype=jnp.int32)[None, :]).astype(jnp.int32)
    before = jnp.cumsum(member, axis=0) - member
    within = jnp.sum(before * member, axis=1)
    target = bins * per_plane + within
    source = (
        jnp.full((slot_total,), count, jnp.int32).at[target].set(jnp.arange(count, dtype=jnp.int32))
    )
    filled = source < count
    picked = jnp.minimum(source, count - 1)
    slot_tile = jnp.where(filled, tiles[picked], tile_count).reshape(planes, per_plane)
    columns = jnp.take(col_weight[0], picked, axis=0).reshape(planes, per_plane, width_v, width_q)
    start = jnp.zeros((tile_count, rows_k * 2 * width_q), jnp.float32)
    rows_sent = jnp.take(row_weight[0], picked, axis=0).reshape(planes, per_plane, rows_k, width_v)
    vis_sent = jnp.take(vis[0], picked, axis=0).reshape(planes, per_plane, 2, width_v)
    got_rows, got_vis, got_columns, got_tiles = (
        lax.all_to_all(rows_sent, "tm", split_axis=0, concat_axis=0, tiled=True),
        lax.all_to_all(vis_sent, "tm", split_axis=0, concat_axis=0, tiled=True),
        lax.all_to_all(columns, "tm", split_axis=0, concat_axis=0, tiled=True),
        lax.all_to_all(slot_tile, "tm", split_axis=0, concat_axis=0, tiled=True),
    )

    def step_raw(total, group):
        rows, visibility, cols, targets = group
        return (grid_group(total, weigh_rows(rows, visibility), cols, targets), None)

    groups = (
        got_rows.reshape(turns, group_len, rows_k, width_v),
        got_vis.reshape(turns, group_len, 2, width_v),
        got_columns.reshape(turns, group_len, width_v, width_q),
        got_tiles.reshape(turns, group_len),
    )
    total, _ = lax.scan(step_raw, start, groups)
    partial_value = total.reshape(tile_count, rows_k, 2 * width_q)
    share = rows_k // lax.axis_size("chan")
    summed = lax.psum(partial_value, "chan")
    mine = lax.dynamic_slice_in_dim(summed, lax.axis_index("chan") * share, share, 1)
    rounded = mine.astype(jnp.bfloat16)
    result = jnp.einsum("tkq,qr->ktr", rounded, w_kernel[0], preferred_element_type=jnp.float32)
    return result[None]


def solution(mesh):
    in_specs = (
        P(("groups", "chan"), "tm", None, None),
        P(("groups", "chan"), "tm", None, None),
        P(("groups", "chan"), "tm", None, None),
        P(("groups", "chan"), "tm", None),
        P(("groups", "chan"), "tm"),
        P(("groups", "tm"), None, None),
    )
    out_specs = P(("groups", "tm"), "chan", None, None)
    return jax.shard_map(body, mesh=mesh, in_specs=in_specs, out_specs=out_specs, check_vma=False)
```

profile of v0, /device:TPU:1, one launch (start us, length us, event | category | flops | bytes accessed | tf_op | source)
XLA Modules:
  0.0 493.3 jit_solution(4983551968529737838)
XLA Ops:
  0.0 0.0 copy-start
  0.0 0.9 fusion.8
  0.9 0.1 reduce_window_sum.11
  0.9 0.8 select_reduce_fusion
  1.8 0.7 fusion.9
  2.4 0.7 scatter_custom_fusion.1
  3.1 1.4 gather_fusion
  4.6 0.7 all_to_all.17
  5.3 5.4 %all-to-all-start = ((s32[4,1,16]{2,1,0:T(1,128)}), s32[4,1,16]{2,1,0:T(1,128)S(1)}, u32[]{:S(2)}, u32[]{:S(2)}) async-start(s32[4,1,16]{2,1,0:T(1,128)} %bitcast.13), calls=%async_computation | async-start | bytes 4096 | tf_op jit(solution)/shard_map/all_to_all | solution.py:53
  10.7 0.1 broadcast_in_dim.53
  10.8 1.4 gather_fusion.3
  12.1 0.8 broadcast_select_fusion.2
  12.9 3.4 gather_fusion.2
  16.3 0.0 all-to-all-done
  16.3 4.5 all-to-all-start.3
  20.8 3.2 broadcast_select_fusion.1
  24.1 1.3 all-to-all-done.3
  25.3 4.4 all-to-all-start.2
  29.8 0.0 copy-done
  29.8 2.8 gather_fusion.1
  32.6 6.4 %copy.14 = bf16[64,128,256]{1,2,0:T(8,128)(2,1)} copy(bf16[64,128,256]{2,1,0:T(8,128)(2,1)} %gather_fusion.1) | data formatting | bytes 8388608 | tf_op jit(solution)/shard_map/jit(_take)/gather | solution.py:45
  39.0 4.6 broadcast_select_fusion
  43.6 34.0 %all-to-all-done.2 = bf16[4,16,128,128]{3,2,1,0:T(8,128)(2,1)} async-done(((bf16[4,16,128,128]{3,2,1,0:T(8,128)(2,1)}), bf16[4,16,128,128]{3,2,1,0:T(8,128)(2,1)}, u32[]{:S(2)}, u32[]{:S(2)}) %all-to-all-start.2) | async-done | bytes 2097184 | tf_op jit(solution)/shard_map/all_to_all | solution.py:50
  77.6 5.0 %all-to-all-start.1 = ((bf16[4,16,128,256]{2,3,1,0:T(8,128)(2,1)}), bf16[4,16,128,256]{2,3,1,0:T(8,128)(2,1)}, u32[]{:S(2)}, u32[]{:S(2)}) async-start(bf16[4,16,128,256]{2,3,1,0:T(8,128)(2,1)} %broadcast_select_fusion), calls=%async_computation.1 | async-start | bytes 8388608 | tf_op jit(solution)/shard_map/all_to_all | solution.py:52
  82.6 92.6 %all-to-all-done.1 = bf16[4,16,128,256]{2,3,1,0:T(8,128)(2,1)} async-done(((bf16[4,16,128,256]{2,3,1,0:T(8,128)(2,1)}), bf16[4,16,128,256]{2,3,1,0:T(8,128)(2,1)}, u32[]{:S(2)}, u32[]{:S(2)}) %all-to-all-start.1) | async-done | bytes 4194336 | tf_op jit(solution)/shard_map/all_to_all | solution.py:52
  175.2 2.2 broadcast_in_dim.50
  177.5 227.6 %while.10 = (s32[]{:T(128)}, f32[16,65536]{1,0:T(8,128)}, s32[4,16]{1,0:T(4,128)S(1)}, bf16[4,16,128,256]{2,3,1,0:T(8,128)(2,1)}, bf16[4,16,128,128]{3,2,1,0:T(8...) while((s32[]{:T(128)}, f32[16,65536]{1,0:T(8,128)}, s32[4,16]{1,0:T(4,128)S(1)}, ...), condition=%wide.region_5.6_spmd, body=%wide.region_3.5_spmd.sunk | while | flops 270798912 | bytes 37266200 | solution.py:66
  177.5 1.1 bitcast_convert_fusion.5
  178.6 3.9 convolution_bitcast_fusion.3
  182.5 7.2 %copy.19 = f32[16,128,2,256]{3,2,1,0:T(2,128)} copy(f32[16,128,2,256]{1,3,2,0:T(8,128)} %convolution_bitcast_fusion.3) | data formatting | bytes 8388608 | tf_op jit(solution)/shard_map/while/body/eval_jaxpr/ghkv,gvq->gkhq/transpose | solution.py:11
  189.7 6.3 %reshape.160 = f32[16,65536]{1,0:T(8,128)} reshape(f32[16,128,2,256]{3,2,1,0:T(2,128)} %copy.19) | data formatting | bytes 8388608 | tf_op jit(solution)/shard_map/while/body/eval_jaxpr/reshape | solution.py:12
  196.1 38.3 %scatter_fusion = f32[16,65536]{1,0:T(8,128)} fusion(f32[16,65536]{1,0:T(8,128)} %get-tuple-element.97, s32[16]{0:T(128)S(1)} %fusion.16, f32[16,65536]{1,0:T(8,128)} %reshape.160), kind=kCustom, calls=%fused_computation.4.clone.1 | custom fusion | flops 1048576 | bytes 12582976 | tf_op jit(solution)/shard_map/while/body/eval_jaxpr/scatter-add | solution.py:13
  234.4 1.1 bitcast_convert_fusion.5
  235.6 3.9 convolution_bitcast_fusion.3
  239.5 7.2 %copy.19 = f32[16,128,2,256]{3,2,1,0:T(2,128)} copy(f32[16,128,2,256]{1,3,2,0:T(8,128)} %convolution_bitcast_fusion.3) | data formatting | bytes 8388608 | tf_op jit(solution)/shard_map/while/body/eval_jaxpr/ghkv,gvq->gkhq/transpose | solution.py:11
  246.7 6.3 %reshape.160 = f32[16,65536]{1,0:T(8,128)} reshape(f32[16,128,2,256]{3,2,1,0:T(2,128)} %copy.19) | data formatting | bytes 8388608 | tf_op jit(solution)/shard_map/while/body/eval_jaxpr/reshape | solution.py:12
  253.0 38.0 %scatter_fusion = f32[16,65536]{1,0:T(8,128)} fusion(f32[16,65536]{1,0:T(8,128)} %get-tuple-element.97, s32[16]{0:T(128)S(1)} %fusion.16, f32[16,65536]{1,0:T(8,128)} %reshape.160), kind=kCustom, calls=%fused_computation.4.clone.1 | custom fusion | flops 1048576 | bytes 12582976 | tf_op jit(solution)/shard_map/while/body/eval_jaxpr/scatter-add | solution.py:13
  291.0 1.1 bitcast_convert_fusion.5
  292.1 3.9 convolution_bitcast_fusion.3
  296.0 7.2 %copy.19 = f32[16,128,2,256]{3,2,1,0:T(2,128)} copy(f32[16,128,2,256]{1,3,2,0:T(8,128)} %convolution_bitcast_fusion.3) | data formatting | bytes 8388608 | tf_op jit(solution)/shard_map/while/body/eval_jaxpr/ghkv,gvq->gkhq/transpose | solution.py:11
  303.2 6.3 %reshape.160 = f32[16,65536]{1,0:T(8,128)} reshape(f32[16,128,2,256]{3,2,1,0:T(2,128)} %copy.19) | data formatting | bytes 8388608 | tf_op jit(solution)/shard_map/while/body/eval_jaxpr/reshape | solution.py:12
  309.6 38.6 %scatter_fusion = f32[16,65536]{1,0:T(8,128)} fusion(f32[16,65536]{1,0:T(8,128)} %get-tuple-element.97, s32[16]{0:T(128)S(1)} %fusion.16, f32[16,65536]{1,0:T(8,128)} %reshape.160), kind=kCustom, calls=%fused_computation.4.clone.1 | custom fusion | flops 1048576 | bytes 12582976 | tf_op jit(solution)/shard_map/while/body/eval_jaxpr/scatter-add | solution.py:13
  348.2 1.1 bitcast_convert_fusion.5
  349.3 3.9 convolution_bitcast_fusion.3
  353.2 7.2 %copy.19 = f32[16,128,2,256]{3,2,1,0:T(2,128)} copy(f32[16,128,2,256]{1,3,2,0:T(8,128)} %convolution_bitcast_fusion.3) | data formatting | bytes 8388608 | tf_op jit(solution)/shard_map/while/body/eval_jaxpr/ghkv,gvq->gkhq/transpose | solution.py:11
  360.4 6.3 %reshape.160 = f32[16,65536]{1,0:T(8,128)} reshape(f32[16,128,2,256]{3,2,1,0:T(2,128)} %copy.19) | data formatting | bytes 8388608 | tf_op jit(solution)/shard_map/while/body/eval_jaxpr/reshape | solution.py:12
  366.8 38.3 %scatter_fusion = f32[16,65536]{1,0:T(8,128)} fusion(f32[16,65536]{1,0:T(8,128)} %get-tuple-element.97, s32[16]{0:T(128)S(1)} %fusion.16, f32[16,65536]{1,0:T(8,128)} %reshape.160), kind=kCustom, calls=%fused_computation.4.clone.1 | custom fusion | flops 1048576 | bytes 12582976 | tf_op jit(solution)/shard_map/while/body/eval_jaxpr/scatter-add | solution.py:13
  405.0 6.5 %copy.17 = f32[2,8,128,512]{3,2,1,0:T(8,128)} copy(f32[2,8,128,512]{3,1,2,0:T(8,128)} %bitcast.63) | data formatting | bytes 8388608
  411.6 0.0 copy-start.1
  411.6 78.7 %all-reduce.1 = bf16[16,128,512]{2,1,0:T(8,128)(2,1)} all-reduce(f32[16,128,512]{2,1,0:T(8,128)} %bitcast.66), channel_id=1, replica_groups=mesh['groups'=2,'tm'=4,'chan'=4] {'chan'}, use_global_device_ids=true, to_apply=%region_6.7 | all-reduce | flops 1048576 | bytes 6291456 | tf_op jit(solution)/shard_map/psum | solution.py:69
  490.2 0.0 copy-done.1
  490.2 1.5 convolution_bitcast_fusion.1
  491.7 1.6 copy.15
  (12 shorter events, 0.1 us)
Async XLA Ops:
  0.0 29.8 %copy-start = (bf16[1,32,128,256]{3,2,1,0:T(8,128)(2,1)S(1)}, bf16[1,32,128,256]{3,2,1,0:T(8,128)(2,1)}, u32[]{:S(2)}) copy-start(bf16[1,32,128,256]{3,2,1,0:T(8,128)(2,1)} %param.10) | copy-start | bytes 6291460
  5.3 11.0 %all-to-all-start = ((s32[4,1,16]{2,1,0:T(1,128)}), s32[4,1,16]{2,1,0:T(1,128)S(1)}, u32[]{:S(2)}, u32[]{:S(2)}) async-start(s32[4,1,16]{2,1,0:T(1,128)} %bitcast.13), calls=%async_computation | async-start | bytes 4096 | tf_op jit(solution)/shard_map/all_to_all | solution.py:53
  16.3 9.0 %all-to-all-start.3 = ((bf16[4,16,2,128]{3,2,1,0:T(2,128)(2,1)}), bf16[4,16,2,128]{3,2,1,0:T(2,128)(2,1)S(1)}, u32[]{:S(2)}, u32[]{:S(2)}) async-start(bf16[4,16,2,128]{3,2,1,0:T(2,128)(2,1)} %broadcast_select_fusion.2), calls=%async_computation.3 | async-start | bytes 65536 | tf_op jit(solution)/shard_map/all_to_all | solution.py:51
  25.3 52.3 %all-to-all-start.2 = ((bf16[4,16,128,128]{3,2,1,0:T(8,128)(2,1)}), bf16[4,16,128,128]{3,2,1,0:T(8,128)(2,1)}, u32[]{:S(2)}, u32[]{:S(2)}) async-start(bf16[4,16,128,128]{3,2,1,0:T(8,128)(2,1)} %broadcast_select_fusion.1), calls=%async_computation.2 | async-start | bytes 4194304 | tf_op jit(solution)/shard_map/all_to_all | solution.py:50
  77.6 97.6 %all-to-all-start.1 = ((bf16[4,16,128,256]{2,3,1,0:T(8,128)(2,1)}), bf16[4,16,128,256]{2,3,1,0:T(8,128)(2,1)}, u32[]{:S(2)}, u32[]{:S(2)}) async-start(bf16[4,16,128,256]{2,3,1,0:T(8,128)(2,1)} %broadcast_select_fusion), calls=%async_computation.1 | async-start | bytes 8388608 | tf_op jit(solution)/shard_map/all_to_all | solution.py:52
  411.6 78.7 %copy-start.1 = (bf16[1,512,512]{2,1,0:T(8,128)(2,1)S(1)}, bf16[1,512,512]{2,1,0:T(8,128)(2,1)}, u32[]{:S(2)}) copy-start(bf16[1,512,512]{2,1,0:T(8,128)(2,1)} %param.13) | copy-start | bytes 1572868
where the time goes:
time: 495 us; the launch traced here: 493 us
  other arithmetic  169 us (34%)
  waiting for transfers between devices  128 us (26%)
  local copies, waits for them, and re-layouts  81.2 us (16%)
  blocking collectives  78.7 us (16%)
  starting transfers between devices  19.4 us (4%)
  matrix products  17.1 us (3%)
    scatter-add x4, other arithmetic, grid_group(): return total.at[targets].add(flat, mode='drop')  153 us
    all_to_all x1, waiting for transfers between devices, body(): lax.all_to_all(columns, 'tm', split_axis=0, concat_axis=0, tiled=True)  92.6 us
    psum x1, blocking collectives, body(): summed = lax.psum(partial_value, 'chan')  78.7 us
    all_to_all x1, waiting for transfers between devices, body(): lax.all_to_all(rows_sent, 'tm', split_axis=0, concat_axis=0, tiled=True)  34 us
    transpose x4, local copies, waits for them, and re-layouts, grid_group(): jnp.einsum('ghkv,gvq->gkhq', weighted, columns, preferred_element_type=jn...  28.8 us
    reshape x4, local copies, waits for them, and re-layouts, grid_group(): flat = patch.reshape(patch.shape[0], -1)  25.2 us
    dot_general x4, matrix products, grid_group(): jnp.einsum('ghkv,gvq->gkhq', weighted, columns, preferred_element_type=jn...  15.7 us
  transfers between devices with their start and end apart: 4, of which 3 were waited for; matrix products, arithmetic and copies ran while one was open for 5% of the time, Pallas kernels for 0%

commit v1 on v0

--- a/solution.py
+++ b/solution.py
@@ -66,7 +66,9 @@
     total, _ = lax.scan(step_raw, start, groups)
     partial_value = total.reshape(tile_count, rows_k, 2 * width_q)
     share = rows_k // lax.axis_size("chan")
-    summed = lax.psum(partial_value, "chan")
+    summed = partial_value
+    for hop in (1, 2):
+        summed = summed + lax.ppermute(summed, "chan", [(dev, dev ^ hop) for dev in range(4)])
     mine = lax.dynamic_slice_in_dim(summed, lax.axis_index("chan") * share, share, 1)
     rounded = mine.astype(jnp.bfloat16)
     result = jnp.einsum("tkq,qr->ktr", rounded, w_kernel[0], preferred_element_type=jnp.float32)

time: 495 us -> 518 us (1.046)
  waiting for transfers between devices: 128 us -> 226 us
  blocking collectives: 78.7 us -> 0 us
    ppermute x0 -> x2, waiting for transfers between devices: none -> 98 us  [body(): lax.ppermute(summed, 'chan', [(dev, dev ^ hop) for dev in range(4)])]
    psum x1 -> x0, blocking collectives: 78.7 us -> none  [body(): summed = lax.psum(partial_value, 'chan')]
  transfers between devices with their start and end apart: 4 -> 6, of which waited for: 3 -> 5; matrix products, arithmetic and copies ran while one was open for 5% -> 4% of each run, Pallas kernels for 0% -> 0%
where the time goes in v1:
time: 518 us; the launch traced here: 515 us
  waiting for transfers between devices  226 us (44%)
  other arithmetic  170 us (33%)
  local copies, waits for them, and re-layouts  79.2 us (15%)
  starting transfers between devices  22.3 us (4%)
  matrix products  17.6 us (3%)
    scatter-add x4, other arithmetic, grid_group(): return total.at[targets].add(flat, mode='drop')  151 us
    ppermute x2, waiting for transfers between devices, body(): lax.ppermute(summed, 'chan', [(dev, dev ^ hop) for dev in range(4)])  98 us
    all_to_all x1, waiting for transfers between devices, body(): lax.all_to_all(columns, 'tm', split_axis=0, concat_axis=0, tiled=True)  92.6 us
    all_to_all x1, waiting for transfers between devices, body(): lax.all_to_all(rows_sent, 'tm', split_axis=0, concat_axis=0, tiled=True)  34 us
    transpose x4, local copies, waits for them, and re-layouts, grid_group(): jnp.einsum('ghkv,gvq->gkhq', weighted, columns, preferred_element_type=jn...  28.8 us
    reshape x4, local copies, waits for them, and re-layouts, grid_group(): flat = patch.reshape(patch.shape[0], -1)  25.2 us
    dot_general x4, matrix products, grid_group(): jnp.einsum('ghkv,gvq->gkhq', weighted, columns, preferred_element_type=jn...  15.7 us
  transfers between devices with their start and end apart: 6, of which 5 were waited for; matrix products, arithmetic and copies ran while one was open for 4% of the time, Pallas kernels for 0%

profile of v1, /device:TPU:1, one launch (start us, length us, event | category | flops | bytes accessed | tf_op | source)
XLA Modules:
  0.0 515.1 jit_solution(18330248097262054838)
XLA Ops:
  0.0 0.0 copy-start
  0.0 0.9 fusion.10
  0.9 0.1 reduce_window_sum.11
  0.9 0.8 select_reduce_fusion
  1.8 0.7 fusion.11
  2.4 0.7 scatter_custom_fusion.1
  3.1 1.4 gather_fusion
  4.6 0.7 all_to_all.17
  5.3 5.4 %all-to-all-start = ((s32[4,1,16]{2,1,0:T(1,128)}), s32[4,1,16]{2,1,0:T(1,128)S(1)}, u32[]{:S(2)}, u32[]{:S(2)}) async-start(s32[4,1,16]{2,1,0:T(1,128)} %bitcast.13), calls=%async_computation | async-start | bytes 4096 | tf_op jit(solution)/shard_map/all_to_all | solution.py:53
  10.7 0.1 broadcast_in_dim.53
  10.8 1.4 gather_fusion.3
  12.1 0.8 broadcast_select_fusion.2
  12.9 3.4 gather_fusion.2
  16.2 0.0 all-to-all-done
  16.2 4.5 all-to-all-start.3
  20.8 3.2 broadcast_select_fusion.1
  24.0 1.3 all-to-all-done.3
  25.3 4.4 all-to-all-start.2
  29.7 0.0 copy-done
  29.7 2.8 gather_fusion.1
  32.5 6.4 %copy.14 = bf16[64,128,256]{1,2,0:T(8,128)(2,1)} copy(bf16[64,128,256]{2,1,0:T(8,128)(2,1)} %gather_fusion.1) | data formatting | bytes 8388608 | tf_op jit(solution)/shard_map/jit(_take)/gather | solution.py:45
  38.9 4.6 broadcast_select_fusion
  43.5 34.0 %all-to-all-done.2 = bf16[4,16,128,128]{3,2,1,0:T(8,128)(2,1)} async-done(((bf16[4,16,128,128]{3,2,1,0:T(8,128)(2,1)}), bf16[4,16,128,128]{3,2,1,0:T(8,128)(2,1)}, u32[]{:S(2)}, u32[]{:S(2)}) %all-to-all-start.2) | async-done | bytes 2097184 | tf_op jit(solution)/shard_map/all_to_all | solution.py:50
  77.5 5.0 all-to-all-start.1
  82.6 92.6 %all-to-all-done.1 = bf16[4,16,128,256]{2,3,1,0:T(8,128)(2,1)} async-done(((bf16[4,16,128,256]{2,3,1,0:T(8,128)(2,1)}), bf16[4,16,128,256]{2,3,1,0:T(8,128)(2,1)}, u32[]{:S(2)}, u32[]{:S(2)}) %all-to-all-start.1) | async-done | bytes 4194336 | tf_op jit(solution)/shard_map/all_to_all | solution.py:52
  175.1 2.2 broadcast_in_dim.50
  177.4 225.7 %while.10 = (s32[]{:T(128)}, f32[16,65536]{1,0:T(8,128)}, s32[4,16]{1,0:T(4,128)S(1)}, bf16[4,16,128,256]{2,3,1,0:T(8,128)(2,1)}, bf16[4,16,128,128]{3,2,1,0:T(8...) while((s32[]{:T(128)}, f32[16,65536]{1,0:T(8,128)}, s32[4,16]{1,0:T(4,128)S(1)}, ...), condition=%wide.region_5.6_spmd, body=%wide.region_3.5_spmd.sunk | while | flops 270798912 | bytes 37266200 | solution.py:66
  177.4 1.1 bitcast_convert_fusion.5
  178.5 3.9 convolution_bitcast_fusion.3
  182.4 7.2 %copy.19 = f32[16,128,2,256]{3,2,1,0:T(2,128)} copy(f32[16,128,2,256]{1,3,2,0:T(8,128)} %convolution_bitcast_fusion.3) | data formatting | bytes 8388608 | tf_op jit(solution)/shard_map/while/body/eval_jaxpr/ghkv,gvq->gkhq/transpose | solution.py:11
  189.6 6.3 %reshape.160 = f32[16,65536]{1,0:T(8,128)} reshape(f32[16,128,2,256]{3,2,1,0:T(2,128)} %copy.19) | data formatting | bytes 8388608 | tf_op jit(solution)/shard_map/while/body/eval_jaxpr/reshape | solution.py:12
  195.9 37.9 %scatter_fusion = f32[16,65536]{1,0:T(8,128)} fusion(f32[16,65536]{1,0:T(8,128)} %get-tuple-element.97, s32[16]{0:T(128)S(1)} %fusion.18, f32[16,65536]{1,0:T(8,128)} %reshape.160), kind=kCustom, calls=%fused_computation.4.clone.1 | custom fusion | flops 1048576 | bytes 12582976 | tf_op jit(solution)/shard_map/while/body/eval_jaxpr/scatter-add | solution.py:13
  233.8 1.1 bitcast_convert_fusion.5
  235.0 3.9 convolution_bitcast_fusion.3
  238.9 7.2 %copy.19 = f32[16,128,2,256]{3,2,1,0:T(2,128)} copy(f32[16,128,2,256]{1,3,2,0:T(8,128)} %convolution_bitcast_fusion.3) | data formatting | bytes 8388608 | tf_op jit(solution)/shard_map/while/body/eval_jaxpr/ghkv,gvq->gkhq/transpose | solution.py:11
  246.1 6.3 %reshape.160 = f32[16,65536]{1,0:T(8,128)} reshape(f32[16,128,2,256]{3,2,1,0:T(2,128)} %copy.19) | data formatting | bytes 8388608 | tf_op jit(solution)/shard_map/while/body/eval_jaxpr/reshape | solution.py:12
  252.4 37.6 %scatter_fusion = f32[16,65536]{1,0:T(8,128)} fusion(f32[16,65536]{1,0:T(8,128)} %get-tuple-element.97, s32[16]{0:T(128)S(1)} %fusion.18, f32[16,65536]{1,0:T(8,128)} %reshape.160), kind=kCustom, calls=%fused_computation.4.clone.1 | custom fusion | flops 1048576 | bytes 12582976 | tf_op jit(solution)/shard_map/while/body/eval_jaxpr/scatter-add | solution.py:13
  290.0 1.1 bitcast_convert_fusion.5
  291.2 3.9 convolution_bitcast_fusion.3
  295.1 7.2 %copy.19 = f32[16,128,2,256]{3,2,1,0:T(2,128)} copy(f32[16,128,2,256]{1,3,2,0:T(8,128)} %convolution_bitcast_fusion.3) | data formatting | bytes 8388608 | tf_op jit(solution)/shard_map/while/body/eval_jaxpr/ghkv,gvq->gkhq/transpose | solution.py:11
  302.3 6.3 %reshape.160 = f32[16,65536]{1,0:T(8,128)} reshape(f32[16,128,2,256]{3,2,1,0:T(2,128)} %copy.19) | data formatting | bytes 8388608 | tf_op jit(solution)/shard_map/while/body/eval_jaxpr/reshape | solution.py:12
  308.6 38.0 %scatter_fusion = f32[16,65536]{1,0:T(8,128)} fusion(f32[16,65536]{1,0:T(8,128)} %get-tuple-element.97, s32[16]{0:T(128)S(1)} %fusion.18, f32[16,65536]{1,0:T(8,128)} %reshape.160), kind=kCustom, calls=%fused_computation.4.clone.1 | custom fusion | flops 1048576 | bytes 12582976 | tf_op jit(solution)/shard_map/while/body/eval_jaxpr/scatter-add | solution.py:13
  346.6 1.1 bitcast_convert_fusion.5
  347.8 3.9 convolution_bitcast_fusion.3
  351.7 7.2 %copy.19 = f32[16,128,2,256]{3,2,1,0:T(2,128)} copy(f32[16,128,2,256]{1,3,2,0:T(8,128)} %convolution_bitcast_fusion.3) | data formatting | bytes 8388608 | tf_op jit(solution)/shard_map/while/body/eval_jaxpr/ghkv,gvq->gkhq/transpose | solution.py:11
  358.9 6.3 %reshape.160 = f32[16,65536]{1,0:T(8,128)} reshape(f32[16,128,2,256]{3,2,1,0:T(2,128)} %copy.19) | data formatting | bytes 8388608 | tf_op jit(solution)/shard_map/while/body/eval_jaxpr/reshape | solution.py:12
  365.2 37.9 %scatter_fusion = f32[16,65536]{1,0:T(8,128)} fusion(f32[16,65536]{1,0:T(8,128)} %get-tuple-element.97, s32[16]{0:T(128)S(1)} %fusion.18, f32[16,65536]{1,0:T(8,128)} %reshape.160), kind=kCustom, calls=%fused_computation.4.clone.1 | custom fusion | flops 1048576 | bytes 12582976 | tf_op jit(solution)/shard_map/while/body/eval_jaxpr/scatter-add | solution.py:13
  403.1 4.6 copy.17
  407.7 0.0 copy-start.1
  407.7 2.0 collective-permute-start
  409.7 6.8 %collective-permute-done = f32[16,128,512]{2,1,0:T(8,128)S(1)} collective-permute-done((f32[16,128,512]{2,1,0:T(8,128)S(1)}, f32[16,128,512]{2,1,0:T(8,128)S(1)}, u32[]{:S(2)}, u32[]{:S(2)}) %collective-permute-start) | collective-permute-done | bytes 4194336 | tf_op jit(solution)/shard_map/ppermute | solution.py:71
  416.5 3.0 bitcast_add_fusion.1
  419.4 0.9 collective-permute-start.1
  420.3 91.2 %collective-permute-done.1 = f32[16,128,512]{2,1,0:T(8,128)} collective-permute-done((f32[16,128,512]{2,1,0:T(8,128)}, f32[16,128,512]{2,1,0:T(8,128)}, u32[]{:S(2)}, u32[]{:S(2)}) %collective-permute-start.1) | collective-permute-done | bytes 4194336 | tf_op jit(solution)/shard_map/ppermute | solution.py:71
  511.5 0.0 copy-done.1
  511.5 2.0 convolution_bitcast_fusion.1
  513.5 1.6 copy.15
  (12 shorter events, 0.1 us)
Async XLA Ops:
  0.0 29.7 %copy-start = (bf16[1,32,128,256]{3,2,1,0:T(8,128)(2,1)S(1)}, bf16[1,32,128,256]{3,2,1,0:T(8,128)(2,1)}, u32[]{:S(2)}) copy-start(bf16[1,32,128,256]{3,2,1,0:T(8,128)(2,1)} %param.10) | copy-start | bytes 6291460
  5.3 11.0 %all-to-all-start = ((s32[4,1,16]{2,1,0:T(1,128)}), s32[4,1,16]{2,1,0:T(1,128)S(1)}, u32[]{:S(2)}, u32[]{:S(2)}) async-start(s32[4,1,16]{2,1,0:T(1,128)} %bitcast.13), calls=%async_computation | async-start | bytes 4096 | tf_op jit(solution)/shard_map/all_to_all | solution.py:53
  16.2 9.0 %all-to-all-start.3 = ((bf16[4,16,2,128]{3,2,1,0:T(2,128)(2,1)}), bf16[4,16,2,128]{3,2,1,0:T(2,128)(2,1)S(1)}, u32[]{:S(2)}, u32[]{:S(2)}) async-start(bf16[4,16,2,128]{3,2,1,0:T(2,128)(2,1)} %broadcast_select_fusion.2), calls=%async_computation.3 | async-start | bytes 65536 | tf_op jit(solution)/shard_map/all_to_all | solution.py:51
  25.3 52.3 %all-to-all-start.2 = ((bf16[4,16,128,128]{3,2,1,0:T(8,128)(2,1)}), bf16[4,16,128,128]{3,2,1,0:T(8,128)(2,1)}, u32[]{:S(2)}, u32[]{:S(2)}) async-start(bf16[4,16,128,128]{3,2,1,0:T(8,128)(2,1)} %broadcast_select_fusion.1), calls=%async_computation.2 | async-start | bytes 4194304 | tf_op jit(solution)/shard_map/all_to_all | solution.py:50
  77.5 97.6 %all-to-all-start.1 = ((bf16[4,16,128,256]{2,3,1,0:T(8,128)(2,1)}), bf16[4,16,128,256]{2,3,1,0:T(8,128)(2,1)}, u32[]{:S(2)}, u32[]{:S(2)}) async-start(bf16[4,16,128,256]{2,3,1,0:T(8,128)(2,1)} %broadcast_select_fusion), calls=%async_computation.1 | async-start | bytes 8388608 | tf_op jit(solution)/shard_map/all_to_all | solution.py:52
  407.7 103.8 %copy-start.1 = (bf16[1,512,512]{2,1,0:T(8,128)(2,1)S(1)}, bf16[1,512,512]{2,1,0:T(8,128)(2,1)}, u32[]{:S(2)}) copy-start(bf16[1,512,512]{2,1,0:T(8,128)(2,1)} %param.13) | copy-start | bytes 1572868
  407.7 8.8 %collective-permute-start = (f32[16,128,512]{2,1,0:T(8,128)S(1)}, f32[16,128,512]{2,1,0:T(8,128)S(1)}, u32[]{:S(2)}, u32[]{:S(2)}) collective-permute-start(f32[16,128,512]{2,1,0:T(8,128)S(1)} %bitcast.66), channel_id=1, source_target_pairs={{0,1},{1,0},{2,3},{3,2},{4,5},{5,4},{6,7},{7,6},{8,9},{9,8},{10,11... | collective-permute-start | bytes 12582920 | tf_op jit(solution)/shard_map/ppermute | solution.py:71
  419.4 92.1 %collective-permute-start.1 = (f32[16,128,512]{2,1,0:T(8,128)}, f32[16,128,512]{2,1,0:T(8,128)}, u32[]{:S(2)}, u32[]{:S(2)}) collective-permute-start(f32[16,128,512]{2,1,0:T(8,128)} %bitcast_add_fusion.1), channel_id=1, source_target_pairs={{0,2},{1,3},{2,0},{3,1},{4,6},{5,7},{6,4},{7,5},{8,10},{9,11},{10,... | collective-permute-start | bytes 12582920 | tf_op jit(solution)/shard_map/ppermute | solution.py:71
